TPU v7x, 32 devices: a whole 2x2x4 slice. The times are simulated.
32 devices in a mesh: turn: 4 (over y, core), blk: 4 (over z), strip: 2 (over x).
Axes of the slice: x: 2, y: 2, z: 4, core: 2. Of those that a mesh axis runs over, the one named last changes fastest.
Arguments:
- echoes: bfloat16 [2, 256, 32768], P(None, 'blk', ('turn', 'strip')), may hold values from -6 to 6
- filters: bfloat16 [2, 8, 32768], P(None, 'blk'), may hold values from -6 to 6
- slab_index: int32 [256], P(('blk', 'turn')), may hold values from 0 to 7
- shifts: int32 [256], P(('blk', 'turn')), may hold values from 0 to 32767
Outputs:
- focused: float32 [2, 256, 32768], P(None, ('blk', 'turn'), 'strip')
All inputs are finite; a program needn't handle non-finite values.
Results may differ from a plain program's by a relative error of at most 0.0003.
Values may be sent and summed in bfloat16 or wider, within the bound.
A program may use at most 128 MiB of HBM per device.

v0:
```python
import functools
import math

import jax
import jax.numpy as jnp
import numpy as np
from jax import lax
from jax.experimental import pallas as pl
from jax.experimental.pallas import tpu as pltpu
from jax.sharding import PartitionSpec as P

LANES = 128
PAIR = 2
MESH = pl.DeviceIdType.MESH
f32, bf16 = jnp.float32, jnp.bfloat16


def split_np(table):
    high = table.astype(jnp.bfloat16)
    low = (table - high.astype(np.float64)).astype(jnp.bfloat16)
    return high, low


def make_tables(length, sources, strips):
    half = LANES
    outer = length // (2 * half)
    local = outer // sources
    a_ids, c_ids = np.arange(outer), np.arange(outer)
    b_ids = np.arange(half)
    tau = np.exp(-2j * np.pi * half * c_ids / length)
    first = np.exp(-2j * np.pi * ((c_ids[:, None] * a_ids[None, :]) % outer) / outer)
    stage_one = []
    for mat in (first, tau[:, None] * first):
        grouped = mat.reshape(outer, sources, 1, local)
        top = np.concatenate([grouped.real, -grouped.imag], 2).reshape(outer, 2 * outer)
        bottom = np.concatenate([grouped.imag, grouped.real], 2).reshape(outer, 2 * outer)
        stage_one.append(np.concatenate(split_np(np.concatenate([top, bottom], 0)), 0))
    stage_one = np.stack(stage_one)
    base = np.exp(-2j * np.pi * ((b_ids[:, None] * b_ids[None, :]) % half) / half)

    def right(mat):
        whole = np.concatenate(
            [np.concatenate([mat.real, mat.imag], 1), np.concatenate([-mat.imag, mat.real], 1)], 0
        )
        high, low = split_np(whole)
        return np.concatenate([high, low, high], 0)

    stage_two = np.stack([right(base), right(base.conj())])
    twist = np.exp(-2j * np.pi * ((c_ids[:, None] * b_ids[None, :]) % length) / length)
    omega = np.exp(-2j * np.pi * b_ids / (2 * half))
    turned = twist * omega[None, :]
    twists = np.stack([twist.real, twist.imag, turned.real, turned.imag]).astype(np.float32)
    rows = outer // strips
    last = []
    for strip in range(strips):
        picked = np.arange(strip * rows, (strip + 1) * rows)
        back = np.exp(2j * np.pi * ((picked[:, None] * c_ids[None, :]) % outer) / outer) / length
        per_half = []
        for mat in (back, back * tau.conj()[None, :]):
            whole = np.concatenate(
                [np.concatenate([mat.real, -mat.imag], 1), np.concatenate([mat.imag, mat.real], 1)], 0
            )
            per_half.append(np.concatenate(split_np(whole), 0))
        last.append(np.stack(per_half))
    return stage_one, stage_two, twists, np.stack(last)


def cosine_sine(phase, length):
    quarter = length // 4
    wrapped = phase & (length - 1)
    quadrant = (wrapped + quarter // 2) // quarter if quarter & (quarter - 1) else (
        wrapped + quarter // 2
    ) >> (quarter.bit_length() - 1)
    angle = (wrapped - quadrant * quarter).astype(f32) * (2.0 * math.pi / length)
    square = angle * angle
    sine = angle * (
        1.0 + square * (-1.0 / 6 + square * (1.0 / 120 + square * (-1.0 / 5040 + square * (1.0 / 362880))))
    )
    cosine = 1.0 + square * (
        -0.5
        + square * (1.0 / 24 + square * (-1.0 / 720 + square * (1.0 / 40320 - square * (1.0 / 3628800))))
    )
    odd = (quadrant & 1) == 1
    out_cos = jnp.where(odd, sine, cosine)
    out_sin = jnp.where(odd, cosine, sine)
    quad = quadrant & 3
    out_cos = jnp.where((quad == 1) | (quad == 2), -out_cos, out_cos)
    out_sin = jnp.where(quad >= 2, -out_sin, out_sin)
    return out_cos, out_sin


def cmul(ar, ai, br, bi):
    return ar * br - ai * bi, ar * bi + ai * br


def split(values):
    high = values.astype(bf16)
    return high, (values - high.astype(f32)).astype(bf16)


def dot(left, right):
    return jnp.dot(left, right, preferred_element_type=f32)


def body(
    turns, blks, strips, length,
    shifts_ref, slabs_ref, ech_ref, filt_ref, one_hbm, two_hbm, twist_hbm, last_hbm,
    out_ref,
    recv, filt_all, inv_twist, ramp, spec, one_ref, two_ref, twist_ref, last_ref, ech_raw, filt_raw, staged, outbox,
    send_sem, recv_sem, fsend, frecv, gsend, grecv, load_sem,
):
    turn, blk, strip = lax.axis_index("turn"), lax.axis_index("blk"), lax.axis_index("strip")
    pairs = recv.shape[0]
    row_count = pairs * PAIR
    slab_local = filt_ref.shape[1] * LANES // length
    core = lax.rem(turn, 2)
    partner = turn + 1 - 2 * core
    peers = [(dt, ds) for dt in range(turns) for ds in range(strips) if (dt, ds) != (0, 0)]

    def peer(dt, ds):
        return (lax.rem(turn + dt, turns), blk, lax.rem(strip + ds, strips))

    me = turn * strips + strip
    twist_load = pltpu.make_async_copy(twist_hbm, twist_ref, load_sem.at[0])
    one_load = pltpu.make_async_copy(one_hbm, one_ref, load_sem.at[1])
    two_load = pltpu.make_async_copy(two_hbm, two_ref, load_sem.at[2])
    last_load = pltpu.make_async_copy(last_hbm.at[strip], last_ref, load_sem.at[3])
    echo_load = pltpu.make_async_copy(ech_ref, ech_raw, load_sem.at[4])
    filter_load = pltpu.make_async_copy(filt_ref, filt_raw, load_sem.at[5])
    echo_load.start()
    filter_load.start()

    barrier = pltpu.get_barrier_semaphore()
    for dt, ds in peers:
        pl.semaphore_signal(barrier, inc=1, device_id=peer(dt, ds), device_id_type=MESH)
    for dz in range(1, blks):
        pl.semaphore_signal(
            barrier, inc=1, device_id=(turn, lax.rem(blk + dz, blks), strip), device_id_type=MESH
        )
    twist_load.start()
    one_load.start()
    two_load.start()
    last_load.start()
    pl.semaphore_wait(barrier, len(peers) + blks - 1)

    def echo_copy(step, dt, ds):
        to = peer(dt, ds)
        return pltpu.make_async_remote_copy(
            src_ref=outbox.at[to[0], step],
            dst_ref=recv.at[step, me],
            send_sem=send_sem.at[step, dt * strips + ds],
            recv_sem=recv_sem.at[step, dt * strips + ds],
            device_id=to,
            device_id_type=MESH,
        )

    def filter_copy(dz):
        return pltpu.make_async_remote_copy(
            src_ref=filt_all.at[pl.ds(blk * slab_local, slab_local), core],
            dst_ref=filt_all.at[pl.ds(blk * slab_local, slab_local), core],
            send_sem=fsend.at[dz],
            recv_sem=frecv.at[dz],
            device_id=(turn, lax.rem(blk + dz, blks), strip),
            device_id_type=MESH,
        )

    def relay_copy(dz):
        origin = lax.rem(blk + blks - dz, blks)
        place = filt_all.at[pl.ds(origin * slab_local, slab_local), core]
        return pltpu.make_async_remote_copy(
            src_ref=place,
            dst_ref=place,
            send_sem=gsend.at[dz],
            recv_sem=grecv.at[dz],
            device_id=(partner, blk, strip),
            device_id_type=MESH,
        )

    half = LANES
    outer = length // (2 * half)
    local = ech_raw.shape[2] // 2
    groups = row_count // 8
    per_group = 8 // PAIR

    def arrange(group):
        def fill(to, carry):
            for part in range(2):
                values = ech_raw[part, to * groups + group].astype(f32)
                staged[part] = values.reshape(2 * local * 8, half)
            for part in range(2):
                for row in range(8):
                    for side in range(2):
                        value = staged[part, pl.ds(side * 8 + row, local, stride=16), :]
                        outbox[
                            to, group * per_group + row // PAIR, part, row % PAIR, :,
                            side * half : (side + 1) * half,
                        ] = value.astype(bf16)
            return carry

        lax.fori_loop(0, turns, fill, 0)
        first, end = group * per_group, (group + 1) * per_group

        def start_step(step, carry):
            for dt, ds in peers:
                echo_copy(step, dt, ds).start()
            return carry

        lax.fori_loop(first, end, start_step, 0)

        def keep(step, carry):
            recv[step, me] = outbox[turn, step]
            return carry

        lax.fori_loop(first, end, keep, 0)

    echo_load.wait()
    arrange(0)
    filter_load.wait()
    bins = filt_raw.shape[1]
    bin_ids = lax.broadcasted_iota(jnp.int32, (bins, half), 0)
    d_ids = lax.broadcasted_iota(jnp.int32, (bins, half), 1)
    for s in range(slab_local):
        for e in range(2):
            picker = (bin_ids == (d_ids * 2 + e) * slab_local + s).astype(f32).astype(bf16)
            for part in range(2):
                got = lax.dot_general(
                    filt_raw[part], picker, (((0,), (0,)), ((), ())), preferred_element_type=f32
                )
                filt_all[blk * slab_local + s, part, e] = got.astype(bf16)
    for dz in range(1, blks):
        filter_copy(dz).start()
    for group in range(1, groups):
        arrange(group)

    c_ids = lax.broadcasted_iota(jnp.int32, (outer, half), 0)
    lane_ids = lax.broadcasted_iota(jnp.int32, (8, 2 * half), 1)
    k_ids = jnp.where(lane_ids >= half, (lane_ids - half) * (2 * outer) + outer, lane_ids * (2 * outer))

    def prepare(row, carry):
        shift = shifts_ref[row]
        vr, vi = cosine_sine(c_ids * shift, length)
        vi = -vi
        for part in range(2):
            tr, ti = twist_ref[2 * part], -twist_ref[2 * part + 1]
            rr, ri = cmul(tr, ti, vr, vi)
            inv_twist[row, 2 * part] = rr
            inv_twist[row, 2 * part + 1] = ri
        ur, ui = cosine_sine(k_ids * shift, length)
        ramp[row, 0] = ur
        ramp[row, 1] = -ui
        return carry

    twist_load.wait()
    lax.fori_loop(0, row_count, prepare, 0)
    one_load.wait()
    two_load.wait()

    def lefts(blocks):
        highs, lows = [], []
        for re, im in blocks:
            high, low = split(jnp.concatenate([re, im], 1))
            highs.append(high)
            lows.append(low)
        high, low = jnp.concatenate(highs, 0), jnp.concatenate(lows, 0)
        return jnp.concatenate([high, high, low], 1)

    def forward(step, carry):
        for dt, ds in peers:
            echo_copy(step, dt, ds).wait_recv()
        rows = [recv[step, :, :, i].reshape(2 * outer, 2 * half) for i in range(PAIR)]
        parts = []
        for side in range(2):
            lanes = slice(side * half, (side + 1) * half)
            res = dot(one_ref[side], jnp.concatenate([r[:, lanes] for r in rows], 1))
            parts.append(res[: 2 * outer] + res[2 * outer :])
        total, differ = parts[0] + parts[1], parts[0] - parts[1]
        blocks = []
        for e, value in enumerate((total, differ)):
            tr, ti = twist_ref[2 * e], twist_ref[2 * e + 1]
            for i in range(PAIR):
                lanes = slice(i * half, (i + 1) * half)
                blocks.append(cmul(value[:outer, lanes], value[outer:, lanes], tr, ti))
        spec[step] = dot(lefts(blocks), two_ref[0])
        return carry

    def inverse(step, carry):
        blocks = []
        for e in range(2):
            lanes = slice(e * half, (e + 1) * half)
            for i in range(PAIR):
                row = step * PAIR + i
                picked = filt_all[slabs_ref[row], :, e].astype(f32)
                ur, ui = ramp[row, 0][:1, lanes], ramp[row, 1][:1, lanes]
                gr, gi = cmul(picked[0], picked[1], ur, ui)
                base = (e * PAIR + i) * outer
                z = spec[step, base : base + outer]
                blocks.append(cmul(z[:, :half], z[:, half:], gr, gi))
        back = dot(lefts(blocks), two_ref[1])
        lows, highs = [], []
        for i in range(PAIR):
            row = step * PAIR + i
            got = []
            for e in range(2):
                base = (e * PAIR + i) * outer
                u = back[base : base + outer]
                got.append(
                    cmul(u[:, :half], u[:, half:], inv_twist[row, 2 * e], inv_twist[row, 2 * e + 1])
                )
            lows.append(jnp.concatenate([got[0][0] + got[1][0], got[0][1] + got[1][1]], 0))
            highs.append(jnp.concatenate([got[0][0] - got[1][0], got[0][1] - got[1][1]], 0))
        rows = outer // strips
        for side, value in enumerate((lows, highs)):
            high, low = split(jnp.concatenate(value, 1))
            left = last_ref[side]
            res = dot(left, high)
            res = res[: 2 * rows] + res[2 * rows :] + dot(left[: 2 * rows], low)
            for i in range(PAIR):
                place = lax.rem(step, 8 // PAIR) * PAIR + i + 8 * side
                for part in range(2):
                    out_ref[part, step // (8 // PAIR), pl.ds(place, rows, stride=16), :] = res[
                        part * rows : (part + 1) * rows, i * half : (i + 1) * half
                    ]
        return carry

    def both(step, carry):
        forward(step, 0)
        inverse(step, 0)
        return carry

    early = pairs // 2
    lax.fori_loop(0, early, forward, 0)
    for dz in range(1, blks):
        filter_copy(dz).wait_recv()
        relay_copy(dz).start()
    for dz in range(1, blks):
        relay_copy(dz).wait_recv()
    last_load.wait()
    lax.fori_loop(0, early, inverse, 0)
    lax.fori_loop(early, pairs, both, 0)

    def end_step(step, carry):
        for dt, ds in peers:
            echo_copy(step, dt, ds).wait_send()
        return carry

    lax.fori_loop(0, pairs, end_step, 0)
    for dz in range(1, blks):
        filter_copy(dz).wait_send()
        relay_copy(dz).wait_send()


def per_device(turns, blks, strips, echoes, filters, slab_index, shifts):
    sources = turns * strips
    length = filters.shape[2]
    half = LANES
    outer = length // (2 * half)
    local = outer // sources
    row_count = slab_index.shape[0]
    slab_local = filters.shape[1]
    pairs = row_count // PAIR
    shaped = echoes.reshape(2, -1, 8, 2 * local, half).transpose(0, 1, 3, 2, 4)
    response = filters.reshape(2, slab_local, 2 * outer, half).transpose(0, 2, 1, 3)
    response = response.reshape(2, -1, half)
    tables = [jnp.asarray(t) for t in make_tables(length, sources, strips)]
    hbm, smem = pl.BlockSpec(memory_space=pltpu.HBM), pl.BlockSpec(memory_space=pltpu.SMEM)
    rows = outer // strips
    image = pl.pallas_call(
        functools.partial(body, turns, blks, strips, length),
        out_shape=jax.ShapeDtypeStruct((2, row_count // 8, rows * 16, half), f32),
        in_specs=[smem, smem] + [hbm] * 6,
        out_specs=pl.BlockSpec(memory_space=pltpu.VMEM),
        scratch_shapes=[
            pltpu.VMEM((pairs, sources, 2, PAIR, local, 2 * half), bf16),
            pltpu.VMEM((slab_local * blks, 2, 2, outer, half), bf16),
            pltpu.VMEM((row_count, 4, outer, half), f32),
            pltpu.VMEM((row_count, 2, 8, 2 * half), f32),
            pltpu.VMEM((pairs, 2 * PAIR * outer, 2 * half), f32),
            pltpu.VMEM(tables[0].shape, bf16),
            pltpu.VMEM(tables[1].shape, bf16),
            pltpu.VMEM(tables[2].shape, f32),
            pltpu.VMEM(tables[3].shape[1:], bf16),
            pltpu.VMEM(shaped.shape, bf16),
            pltpu.VMEM(response.shape, bf16),
            pltpu.VMEM((2, 16 * local, half), f32),
            pltpu.VMEM((turns, pairs, 2, PAIR, local, 2 * half), bf16),
            pltpu.SemaphoreType.DMA((pairs, sources)),
            pltpu.SemaphoreType.DMA((pairs, sources)),
            pltpu.SemaphoreType.DMA((blks,)),
            pltpu.SemaphoreType.DMA((blks,)),
            pltpu.SemaphoreType.DMA((blks,)),
            pltpu.SemaphoreType.DMA((blks,)),
            pltpu.SemaphoreType.DMA((6,)),
        ],
        compiler_params=pltpu.CompilerParams(
            collective_id=0, has_side_effects=True, vmem_limit_bytes=56 * 1024 * 1024
        ),
    )(shifts, slab_index, shaped, response, *tables)
    image = image.reshape(2, row_count // 8, rows * 2, 8, half).transpose(0, 1, 3, 2, 4)
    return image.reshape(2, row_count, rows * 2 * half)


def solution(mesh):
    in_specs = (
        P(None, "blk", ("turn", "strip")),
        P(None, "blk", None),
        P(("blk", "turn")),
        P(("blk", "turn")),
    )
    out_specs = P(None, ("blk", "turn"), "strip")
    local = functools.partial(
        per_device, mesh.shape["turn"], mesh.shape["blk"], mesh.shape["strip"]
    )
    return jax.shard_map(local, mesh=mesh, in_specs=in_specs, out_specs=out_specs, check_vma=False)
```

profile of v0, /device:TPU:0, one launch (start us, length us, event | category | flops | bytes accessed | tf_op | source)
XLA Modules:
  0.0 38.9 jit_solution(12800881185762003782)
XLA Ops:
  0.0 35.8 %shard_map.82 = f32[2,2,1024,128]{3,2,1,0:T(8,128)} custom-call(s32[16]{0:T(128)} %shifts_ref.1, s32[16]{0:T(128)} %slabs_ref.1, bf16[2,8,32,8,128]{4,3,2,1,0:T(8,128)(2,1)} %bitcast.14, bf16[2,512,128]{2,1,0:T(8,128)(2,1)} %bitcast.15, bf16[2,512,256]{2,1,0:T(8,128)(2,1)} %constant.8.clone.one_hbm, bf16[2,768,256]{2,1,0:T(8,128)(2,1)} %constant.9.clone.two_hbm, ...), custom_call_target="tpu_custom_call" | custom-call | tf_op jit(solution)/shard_map/pallas_call | solution.py:367
  35.8 3.0 %copy.11 = f32[2,16,16384]{2,1,0:T(8,128)} copy(f32[2,16,16384]{2,1,0:T(8,128)} %bitcast.13) | data formatting | bytes 4194304
where the time goes:
time: 39 us; the launch traced here: 38.9 us
  Pallas kernels  35.8 us (92%)
  local copies, waits for them, and re-layouts  3.05 us (8%)
    pallas_call x1, Pallas kernels, per_device(): pl.pallas_call(functools.partial(body, turns, blks, strips, length), out_...  35.8 us
    unnamed x1, local copies, waits for them, and re-layouts  3.05 us

commit v1 on v0

--- a/solution.py
+++ b/solution.py
@@ -366,7 +366,7 @@
     rows = outer // strips
     image = pl.pallas_call(
         functools.partial(body, turns, blks, strips, length),
-        out_shape=jax.ShapeDtypeStruct((2, row_count // 8, rows * 16, half), f32),
+        out_shape=pltpu.VMEM((2, row_count // 8, rows * 16, half), f32),
         in_specs=[smem, smem] + [hbm] * 6,
         out_specs=pl.BlockSpec(memory_space=pltpu.VMEM),
         scratch_shapes=[

time: 39 us -> 36 us (0.923)
  local copies, waits for them, and re-layouts: 3.05 us -> 1.32 us
  Pallas kernels: 35.8 us -> 34.5 us
    unnamed x1, local copies, waits for them, and re-layouts: 3.05 us -> 1.32 us
    pallas_call x1, Pallas kernels: 35.8 us -> 34.5 us  [per_device(): pl.pallas_call(functools.partial(body, turns, blks, strips, length), out_...]
where the time goes in v1:
time: 36 us; the launch traced here: 35.8 us
  Pallas kernels  34.5 us (96%)
  local copies, waits for them, and re-layouts  1.32 us (4%)
    pallas_call x1, Pallas kernels, per_device(): pl.pallas_call(functools.partial(body, turns, blks, strips, length), out_...  34.5 us
    unnamed x1, local copies, waits for them, and re-layouts  1.32 us

profile of v1, /device:TPU:0, one launch (start us, length us, event | category | flops | bytes accessed | tf_op | source)
XLA Modules:
  0.0 35.8 jit_solution(8022041307103254019)
XLA Ops:
  0.0 34.5 %shard_map.82 = f32[2,2,1024,128]{3,2,1,0:T(8,128)S(1)} custom-call(s32[16]{0:T(128)} %shifts_ref.1, s32[16]{0:T(128)} %slabs_ref.1, bf16[2,8,32,8,128]{4,3,2,1,0:T(8,128)(2,1)} %bitcast.14, bf16[2,512,128]{2,1,0:T(8,128)(2,1)} %bitcast.15, bf16[2,512,256]{2,1,0:T(8,128)(2,1)} %constant.8.clone.one_hbm, bf16[2,768,256]{2,1,0:T(8,128)(2,1)} %constant.9.clone.two_hbm, ...), custom_call_target="tpu_custom_call" | custom-call | tf_op jit(solution)/shard_map/pallas_call | solution.py:367
  34.5 1.3 %copy.11 = f32[2,16,16384]{2,1,0:T(8,128)} copy(f32[2,16,16384]{2,1,0:T(8,128)S(1)} %bitcast.13) | data formatting | bytes 4194304

commit v2 on v1

--- a/solution.py
+++ b/solution.py
@@ -133,15 +133,13 @@
     barrier = pltpu.get_barrier_semaphore()
     for dt, ds in peers:
         pl.semaphore_signal(barrier, inc=1, device_id=peer(dt, ds), device_id_type=MESH)
-    for dz in range(1, blks):
-        pl.semaphore_signal(
-            barrier, inc=1, device_id=(turn, lax.rem(blk + dz, blks), strip), device_id_type=MESH
-        )
     twist_load.start()
     one_load.start()
     two_load.start()
     last_load.start()
-    pl.semaphore_wait(barrier, len(peers) + blks - 1)
+
+    def signal_blk(to):
+        pl.semaphore_signal(barrier, inc=1, device_id=(turn, to, strip), device_id_type=MESH)
 
     def echo_copy(step, dt, ds):
         to = peer(dt, ds)
@@ -198,6 +196,8 @@
             return carry
 
         lax.fori_loop(0, turns, fill, 0)
+
+    def send(group):
         first, end = group * per_group, (group + 1) * per_group
 
         def start_step(step, carry):
@@ -215,6 +215,20 @@
 
     echo_load.wait()
     arrange(0)
+    pl.semaphore_wait(barrier, len(peers) + jnp.where(blk > 0, 1, 0))
+    send(0)
+
+    @pl.when(blk < blks - 1)
+    def _():
+        signal_blk(blk + 1)
+
+    @pl.when(blk == blks - 1)
+    def _():
+        signal_blk(blk - 1)
+
+    for group in range(1, groups):
+        arrange(group)
+        send(group)
     filter_load.wait()
     bins = filt_raw.shape[1]
     bin_ids = lax.broadcasted_iota(jnp.int32, (bins, half), 0)
@@ -228,9 +242,10 @@
                 )
                 filt_all[blk * slab_local + s, part, e] = got.astype(bf16)
     for dz in range(1, blks):
-        filter_copy(dz).start()
-    for group in range(1, groups):
-        arrange(group)
+
+        @pl.when(blk + dz >= blks)
+        def _(dz=dz):
+            filter_copy(dz).start()
 
     c_ids = lax.broadcasted_iota(jnp.int32, (outer, half), 0)
     lane_ids = lax.broadcasted_iota(jnp.int32, (8, 2 * half), 1)
@@ -250,8 +265,23 @@
         ramp[row, 1] = -ui
         return carry
 
+    @pl.when(blk < blks - 1)
+    def _():
+        pl.semaphore_wait(barrier, 1)
+
+        @pl.when(blk > 0)
+        def _():
+            signal_blk(blk - 1)
+
+        for dz in range(1, blks):
+
+            @pl.when(blk + dz < blks)
+            def _(dz=dz):
+                filter_copy(dz).start()
+
     twist_load.wait()
     lax.fori_loop(0, row_count, prepare, 0)
+
     one_load.wait()
     two_load.wait()
 

time: 36 us -> 34 us (0.944)
  Pallas kernels: 34.5 us -> 32.3 us
    pallas_call x1, Pallas kernels: 34.5 us -> 32.3 us  [per_device(): pl.pallas_call(functools.partial(body, turns, blks, strips, length), out_...]
where the time goes in v2:
time: 34 us; the launch traced here: 33.6 us
  Pallas kernels  32.3 us (95%)
  local copies, waits for them, and re-layouts  1.32 us (4%)
    pallas_call x1, Pallas kernels, per_device(): pl.pallas_call(functools.partial(body, turns, blks, strips, length), out_...  32.3 us
    unnamed x1, local copies, waits for them, and re-layouts  1.32 us

profile of v2, /device:TPU:0, one launch (start us, length us, event | category | flops | bytes accessed | tf_op | source)
XLA Modules:
  0.0 33.6 jit_solution(3705235649915500457)
XLA Ops:
  0.0 32.3 %shard_map.82 = f32[2,2,1024,128]{3,2,1,0:T(8,128)S(1)} custom-call(s32[16]{0:T(128)} %shifts_ref.1, s32[16]{0:T(128)} %slabs_ref.1, bf16[2,8,32,8,128]{4,3,2,1,0:T(8,128)(2,1)} %bitcast.14, bf16[2,512,128]{2,1,0:T(8,128)(2,1)} %bitcast.15, bf16[2,512,256]{2,1,0:T(8,128)(2,1)} %constant.8.clone.one_hbm, bf16[2,768,256]{2,1,0:T(8,128)(2,1)} %constant.9.clone.two_hbm, ...), custom_call_target="tpu_custom_call" | custom-call | tf_op jit(solution)/shard_map/pallas_call | solution.py:397
  32.3 1.3 %copy.11 = f32[2,16,16384]{2,1,0:T(8,128)} copy(f32[2,16,16384]{2,1,0:T(8,128)S(1)} %bitcast.13) | data formatting | bytes 4194304

commit v3 on v2

--- a/solution.py
+++ b/solution.py
@@ -146,8 +146,8 @@
         return pltpu.make_async_remote_copy(
             src_ref=outbox.at[to[0], step],
             dst_ref=recv.at[step, me],
-            send_sem=send_sem.at[step, dt * strips + ds],
-            recv_sem=recv_sem.at[step, dt * strips + ds],
+            send_sem=send_sem.at[0],
+            recv_sem=recv_sem.at[step],
             device_id=to,
             device_id_type=MESH,
         )
@@ -156,7 +156,7 @@
         return pltpu.make_async_remote_copy(
             src_ref=filt_all.at[pl.ds(blk * slab_local, slab_local), core],
             dst_ref=filt_all.at[pl.ds(blk * slab_local, slab_local), core],
-            send_sem=fsend.at[dz],
+            send_sem=fsend.at[0],
             recv_sem=frecv.at[dz],
             device_id=(turn, lax.rem(blk + dz, blks), strip),
             device_id_type=MESH,
@@ -168,8 +168,8 @@
         return pltpu.make_async_remote_copy(
             src_ref=place,
             dst_ref=place,
-            send_sem=gsend.at[dz],
-            recv_sem=grecv.at[dz],
+            send_sem=gsend.at[0],
+            recv_sem=grecv.at[0],
             device_id=(partner, blk, strip),
             device_id_type=MESH,
         )
@@ -295,8 +295,8 @@
         return jnp.concatenate([high, high, low], 1)
 
     def forward(step, carry):
-        for dt, ds in peers:
-            echo_copy(step, dt, ds).wait_recv()
+        arrived = recv.at[step, pl.ds(0, len(peers))]
+        pltpu.make_async_copy(arrived, arrived, recv_sem.at[step]).wait()
         rows = [recv[step, :, :, i].reshape(2 * outer, 2 * half) for i in range(PAIR)]
         parts = []
         for side in range(2):
@@ -362,21 +362,16 @@
     for dz in range(1, blks):
         filter_copy(dz).wait_recv()
         relay_copy(dz).start()
-    for dz in range(1, blks):
-        relay_copy(dz).wait_recv()
+    others = filt_all.at[pl.ds(0, (blks - 1) * slab_local), 0]
+    pltpu.make_async_copy(others, others, grecv.at[0]).wait()
     last_load.wait()
     lax.fori_loop(0, early, inverse, 0)
     lax.fori_loop(early, pairs, both, 0)
 
-    def end_step(step, carry):
-        for dt, ds in peers:
-            echo_copy(step, dt, ds).wait_send()
-        return carry
-
-    lax.fori_loop(0, pairs, end_step, 0)
-    for dz in range(1, blks):
-        filter_copy(dz).wait_send()
-        relay_copy(dz).wait_send()
+    sent = recv.at[:, pl.ds(0, len(peers))]
+    pltpu.make_async_copy(sent, sent, send_sem.at[0]).wait()
+    pltpu.make_async_copy(others, others, fsend.at[0]).wait()
+    pltpu.make_async_copy(others, others, gsend.at[0]).wait()
 
 
 def per_device(turns, blks, strips, echoes, filters, slab_index, shifts):
@@ -413,12 +408,12 @@
             pltpu.VMEM(response.shape, bf16),
             pltpu.VMEM((2, 16 * local, half), f32),
             pltpu.VMEM((turns, pairs, 2, PAIR, local, 2 * half), bf16),
-            pltpu.SemaphoreType.DMA((pairs, sources)),
-            pltpu.SemaphoreType.DMA((pairs, sources)),
+            pltpu.SemaphoreType.DMA((1,)),
+            pltpu.SemaphoreType.DMA((pairs,)),
+            pltpu.SemaphoreType.DMA((1,)),
             pltpu.SemaphoreType.DMA((blks,)),
-            pltpu.SemaphoreType.DMA((blks,)),
-            pltpu.SemaphoreType.DMA((blks,)),
-            pltpu.SemaphoreType.DMA((blks,)),
+            pltpu.SemaphoreType.DMA((1,)),
+            pltpu.SemaphoreType.DMA((1,)),
             pltpu.SemaphoreType.DMA((6,)),
         ],
         compiler_params=pltpu.CompilerParams(

time: 34 us -> 32.6 us (0.959)
  Pallas kernels: 32.3 us -> 31 us
    pallas_call x1, Pallas kernels: 32.3 us -> 31 us  [per_device(): pl.pallas_call(functools.partial(body, turns, blks, strips, length), out_...]
where the time goes in v3:
time: 32.6 us; the launch traced here: 32.4 us
  Pallas kernels  31 us (95%)
  local copies, waits for them, and re-layouts  1.32 us (4%)
    pallas_call x1, Pallas kernels, per_device(): pl.pallas_call(functools.partial(body, turns, blks, strips, length), out_...  31 us
    unnamed x1, local copies, waits for them, and re-layouts  1.32 us

profile of v3, /device:TPU:0, one launch (start us, length us, event | category | flops | bytes accessed | tf_op | source)
XLA Modules:
  0.0 32.4 jit_solution(4411853734130497719)
XLA Ops:
  0.0 31.0 %shard_map.82 = f32[2,2,1024,128]{3,2,1,0:T(8,128)S(1)} custom-call(s32[16]{0:T(128)} %shifts_ref.1, s32[16]{0:T(128)} %slabs_ref.1, bf16[2,8,32,8,128]{4,3,2,1,0:T(8,128)(2,1)} %bitcast.14, bf16[2,512,128]{2,1,0:T(8,128)(2,1)} %bitcast.15, bf16[2,512,256]{2,1,0:T(8,128)(2,1)} %constant.8.clone.one_hbm, bf16[2,768,256]{2,1,0:T(8,128)(2,1)} %constant.9.clone.two_hbm, ...), custom_call_target="tpu_custom_call" | custom-call | tf_op jit(solution)/shard_map/pallas_call | solution.py:392
  31.0 1.3 %copy.11 = f32[2,16,16384]{2,1,0:T(8,128)} copy(f32[2,16,16384]{2,1,0:T(8,128)S(1)} %bitcast.13) | data formatting | bytes 4194304

commit v4 on v3

--- a/solution.py
+++ b/solution.py
@@ -11,6 +11,7 @@
 
 LANES = 128
 PAIR = 2
+CHUNK = 64
 MESH = pl.DeviceIdType.MESH
 f32, bf16 = jnp.float32, jnp.bfloat16
 
@@ -32,9 +33,10 @@
     stage_one = []
     for mat in (first, tau[:, None] * first):
         grouped = mat.reshape(outer, sources, 1, local)
-        top = np.concatenate([grouped.real, -grouped.imag], 2).reshape(outer, 2 * outer)
-        bottom = np.concatenate([grouped.imag, grouped.real], 2).reshape(outer, 2 * outer)
-        stage_one.append(np.concatenate(split_np(np.concatenate([top, bottom], 0)), 0))
+        top = np.concatenate([grouped.real, -grouped.imag], 2).reshape(-1, CHUNK, 2 * outer)
+        bottom = np.concatenate([grouped.imag, grouped.real], 2).reshape(-1, CHUNK, 2 * outer)
+        whole = np.concatenate([top, bottom], 1).reshape(2 * outer, 2 * outer)
+        stage_one.append(np.concatenate(split_np(whole), 1))
     stage_one = np.stack(stage_one)
     base = np.exp(-2j * np.pi * ((b_ids[:, None] * b_ids[None, :]) % half) / half)
 
@@ -60,7 +62,8 @@
             whole = np.concatenate(
                 [np.concatenate([mat.real, -mat.imag], 1), np.concatenate([mat.imag, mat.real], 1)], 0
             )
-            per_half.append(np.concatenate(split_np(whole), 0))
+            high, low = split_np(whole)
+            per_half.append(np.concatenate([high, low, high], 1))
         last.append(np.stack(per_half))
     return stage_one, stage_two, twists, np.stack(last)
 
@@ -106,7 +109,7 @@
     turns, blks, strips, length,
     shifts_ref, slabs_ref, ech_ref, filt_ref, one_hbm, two_hbm, twist_hbm, last_hbm,
     out_ref,
-    recv, filt_all, inv_twist, ramp, spec, one_ref, two_ref, twist_ref, last_ref, ech_raw, filt_raw, staged, outbox,
+    recv, filt_all, inv_twist, ramp, spec, middle, one_ref, two_ref, twist_ref, last_ref, ech_raw, filt_raw, staged, outbox,
     send_sem, recv_sem, fsend, frecv, gsend, grecv, load_sem,
 ):
     turn, blk, strip = lax.axis_index("turn"), lax.axis_index("blk"), lax.axis_index("strip")
@@ -115,10 +118,14 @@
     slab_local = filt_ref.shape[1] * LANES // length
     core = lax.rem(turn, 2)
     partner = turn + 1 - 2 * core
-    peers = [(dt, ds) for dt in range(turns) for ds in range(strips) if (dt, ds) != (0, 0)]
+    peers = [
+        (dt, ds) for dt in range(turns) for ds in range(strips) if (dt, ds) != (0, 0)
+    ]
+    peers.sort(key=lambda p: (p[1] == 0, p[0] < 2, p))
 
     def peer(dt, ds):
-        return (lax.rem(turn + dt, turns), blk, lax.rem(strip + ds, strips))
+        to = lax.rem(turn - core + (dt // 2) * 2, turns) + lax.rem(core + dt, 2)
+        return (to, blk, lax.rem(strip + ds, strips))
 
     me = turn * strips + strip
     twist_load = pltpu.make_async_copy(twist_hbm, twist_ref, load_sem.at[0])
@@ -226,9 +233,6 @@
     def _():
         signal_blk(blk - 1)
 
-    for group in range(1, groups):
-        arrange(group)
-        send(group)
     filter_load.wait()
     bins = filt_raw.shape[1]
     bin_ids = lax.broadcasted_iota(jnp.int32, (bins, half), 0)
@@ -247,6 +251,9 @@
         def _(dz=dz):
             filter_copy(dz).start()
 
+    for group in range(1, groups):
+        arrange(group)
+        send(group)
     c_ids = lax.broadcasted_iota(jnp.int32, (outer, half), 0)
     lane_ids = lax.broadcasted_iota(jnp.int32, (8, 2 * half), 1)
     k_ids = jnp.where(lane_ids >= half, (lane_ids - half) * (2 * outer) + outer, lane_ids * (2 * outer))
@@ -294,56 +301,73 @@
         high, low = jnp.concatenate(highs, 0), jnp.concatenate(lows, 0)
         return jnp.concatenate([high, high, low], 1)
 
+    chunks = outer // CHUNK
+
     def forward(step, carry):
         arrived = recv.at[step, pl.ds(0, len(peers))]
         pltpu.make_async_copy(arrived, arrived, recv_sem.at[step]).wait()
         rows = [recv[step, :, :, i].reshape(2 * outer, 2 * half) for i in range(PAIR)]
-        parts = []
+        rights = []
         for side in range(2):
             lanes = slice(side * half, (side + 1) * half)
-            res = dot(one_ref[side], jnp.concatenate([r[:, lanes] for r in rows], 1))
-            parts.append(res[: 2 * outer] + res[2 * outer :])
-        total, differ = parts[0] + parts[1], parts[0] - parts[1]
-        blocks = []
-        for e, value in enumerate((total, differ)):
-            tr, ti = twist_ref[2 * e], twist_ref[2 * e + 1]
-            for i in range(PAIR):
-                lanes = slice(i * half, (i + 1) * half)
-                blocks.append(cmul(value[:outer, lanes], value[outer:, lanes], tr, ti))
-        spec[step] = dot(lefts(blocks), two_ref[0])
+            right = jnp.concatenate([r[:, lanes] for r in rows], 1)
+            rights.append(jnp.concatenate([right, right], 0))
+        for chunk in range(chunks):
+            ids = slice(chunk * CHUNK, (chunk + 1) * CHUNK)
+            even, odd = [
+                dot(one_ref[side, 2 * chunk * CHUNK : 2 * (chunk + 1) * CHUNK], rights[side])
+                for side in range(2)
+            ]
+            blocks = []
+            for e, value in enumerate((even + odd, even - odd)):
+                tr, ti = twist_ref[2 * e, ids], twist_ref[2 * e + 1, ids]
+                for i in range(PAIR):
+                    lanes = slice(i * half, (i + 1) * half)
+                    blocks.append(cmul(value[:CHUNK, lanes], value[CHUNK:, lanes], tr, ti))
+            spec[step, chunk] = dot(lefts(blocks), two_ref[0])
         return carry
 
     def inverse(step, carry):
-        blocks = []
-        for e in range(2):
-            lanes = slice(e * half, (e + 1) * half)
+        for chunk in range(chunks):
+            ids = slice(chunk * CHUNK, (chunk + 1) * CHUNK)
+            blocks = []
+            for e in range(2):
+                lanes = slice(e * half, (e + 1) * half)
+                for i in range(PAIR):
+                    row = step * PAIR + i
+                    picked = filt_all[slabs_ref[row], :, e, ids].astype(f32)
+                    ur, ui = ramp[row, 0][:1, lanes], ramp[row, 1][:1, lanes]
+                    gr, gi = cmul(picked[0], picked[1], ur, ui)
+                    base = (e * PAIR + i) * CHUNK
+                    z = spec[step, chunk, base : base + CHUNK]
+                    blocks.append(cmul(z[:, :half], z[:, half:], gr, gi))
+            back = dot(lefts(blocks), two_ref[1])
             for i in range(PAIR):
                 row = step * PAIR + i
-                picked = filt_all[slabs_ref[row], :, e].astype(f32)
-                ur, ui = ramp[row, 0][:1, lanes], ramp[row, 1][:1, lanes]
-                gr, gi = cmul(picked[0], picked[1], ur, ui)
-                base = (e * PAIR + i) * outer
-                z = spec[step, base : base + outer]
-                blocks.append(cmul(z[:, :half], z[:, half:], gr, gi))
-        back = dot(lefts(blocks), two_ref[1])
-        lows, highs = [], []
-        for i in range(PAIR):
-            row = step * PAIR + i
-            got = []
-            for e in range(2):
-                base = (e * PAIR + i) * outer
-                u = back[base : base + outer]
-                got.append(
-                    cmul(u[:, :half], u[:, half:], inv_twist[row, 2 * e], inv_twist[row, 2 * e + 1])
-                )
-            lows.append(jnp.concatenate([got[0][0] + got[1][0], got[0][1] + got[1][1]], 0))
-            highs.append(jnp.concatenate([got[0][0] - got[1][0], got[0][1] - got[1][1]], 0))
+                got = []
+                for e in range(2):
+                    base = (e * PAIR + i) * CHUNK
+                    u = back[base : base + CHUNK]
+                    got.append(
+                        cmul(
+                            u[:, :half], u[:, half:],
+                            inv_twist[row, 2 * e, ids], inv_twist[row, 2 * e + 1, ids],
+                        )
+                    )
+                lanes = slice(i * half, (i + 1) * half)
+                for part in range(2):
+                    to = slice(part * outer + chunk * CHUNK, part * outer + (chunk + 1) * CHUNK)
+                    for side, value in enumerate((got[0][part] + got[1][part], got[0][part] - got[1][part])):
+                        high, low = split(value)
+                        middle[side, 0, to, lanes] = high
+                        middle[side, 1, to, lanes] = low
+        return lax.fori_loop(step, step + 1, inverse_two, carry)
+
+    def inverse_two(step, carry):
         rows = outer // strips
-        for side, value in enumerate((lows, highs)):
-            high, low = split(jnp.concatenate(value, 1))
-            left = last_ref[side]
-            res = dot(left, high)
-            res = res[: 2 * rows] + res[2 * rows :] + dot(left[: 2 * rows], low)
+        for side in range(2):
+            high, low = middle[side, 0], middle[side, 1]
+            res = dot(last_ref[side], jnp.concatenate([high, high, low], 0))
             for i in range(PAIR):
                 place = lax.rem(step, 8 // PAIR) * PAIR + i + 8 * side
                 for part in range(2):
@@ -358,10 +382,17 @@
         return carry
 
     early = pairs // 2
-    lax.fori_loop(0, early, forward, 0)
-    for dz in range(1, blks):
+    def pass_on(j):
+        origin = jnp.where(blk + j < blks, blk + j, blks - 1 - j)
+        dz = lax.rem(blk - origin + blks, blks)
         filter_copy(dz).wait_recv()
         relay_copy(dz).start()
+
+    lax.fori_loop(0, early - 1, forward, 0)
+    for j in range(1, blks - 1):
+        pass_on(j)
+    lax.fori_loop(early - 1, early, forward, 0)
+    pass_on(blks - 1)
     others = filt_all.at[pl.ds(0, (blks - 1) * slab_local), 0]
     pltpu.make_async_copy(others, others, grecv.at[0]).wait()
     last_load.wait()
@@ -399,7 +430,8 @@
             pltpu.VMEM((slab_local * blks, 2, 2, outer, half), bf16),
             pltpu.VMEM((row_count, 4, outer, half), f32),
             pltpu.VMEM((row_count, 2, 8, 2 * half), f32),
-            pltpu.VMEM((pairs, 2 * PAIR * outer, 2 * half), f32),
+            pltpu.VMEM((pairs, outer // CHUNK, 2 * PAIR * CHUNK, 2 * half), f32),
+            pltpu.VMEM((2, 2, 2 * outer, 2 * half), bf16),
             pltpu.VMEM(tables[0].shape, bf16),
             pltpu.VMEM(tables[1].shape, bf16),
             pltpu.VMEM(tables[2].shape, f32),

time: 32.6 us -> 31.6 us (0.969)
  Pallas kernels: 31 us -> 29.8 us
    pallas_call x1, Pallas kernels: 31 us -> 29.8 us  [per_device(): pl.pallas_call(functools.partial(body, turns, blks, strips, length), out_...]
where the time goes in v4:
time: 31.6 us; the launch traced here: 31.1 us
  Pallas kernels  29.8 us (94%)
  local copies, waits for them, and re-layouts  1.32 us (4%)
    pallas_call x1, Pallas kernels, per_device(): pl.pallas_call(functools.partial(body, turns, blks, strips, length), out_...  29.8 us
    unnamed x1, local copies, waits for them, and re-layouts  1.32 us

profile of v4, /device:TPU:0, one launch (start us, length us, event | category | flops | bytes accessed | tf_op | source)
XLA Modules:
  0.0 31.1 jit_solution(8632628653098732937)
XLA Ops:
  0.0 29.8 %shard_map.82 = f32[2,2,1024,128]{3,2,1,0:T(8,128)S(1)} custom-call(s32[16]{0:T(128)} %shifts_ref.1, s32[16]{0:T(128)} %slabs_ref.1, bf16[2,8,32,8,128]{4,3,2,1,0:T(8,128)(2,1)} %bitcast.14, bf16[2,512,128]{2,1,0:T(8,128)(2,1)} %bitcast.15, bf16[2,256,512]{2,1,0:T(8,128)(2,1)} %constant.8.clone.one_hbm, bf16[2,768,256]{2,1,0:T(8,128)(2,1)} %constant.9.clone.two_hbm, ...), custom_call_target="tpu_custom_call" | custom-call | tf_op jit(solution)/shard_map/pallas_call | solution.py:423
  29.8 1.3 %copy.11 = f32[2,16,16384]{2,1,0:T(8,128)} copy(f32[2,16,16384]{2,1,0:T(8,128)S(1)} %bitcast.13) | data formatting | bytes 4194304

commit v5 on v4

--- a/solution.py
+++ b/solution.py
@@ -12,6 +12,7 @@
 LANES = 128
 PAIR = 2
 CHUNK = 64
+BACK = 32
 MESH = pl.DeviceIdType.MESH
 f32, bf16 = jnp.float32, jnp.bfloat16
 
@@ -132,19 +133,23 @@
     one_load = pltpu.make_async_copy(one_hbm, one_ref, load_sem.at[1])
     two_load = pltpu.make_async_copy(two_hbm, two_ref, load_sem.at[2])
     last_load = pltpu.make_async_copy(last_hbm.at[strip], last_ref, load_sem.at[3])
-    echo_load = pltpu.make_async_copy(ech_ref, ech_raw, load_sem.at[4])
     filter_load = pltpu.make_async_copy(filt_ref, filt_raw, load_sem.at[5])
-    echo_load.start()
+    groups = row_count // 8
+    per_group = 8 // PAIR
+
+    def load_group(group):
+        for to in range(turns):
+            block = pl.ds(to * groups + group, 1)
+            pltpu.make_async_copy(
+                ech_ref.at[:, block], ech_raw.at[:, block], load_sem.at[6 + group]
+            ).start()
+
+    load_group(0)
     filter_load.start()
 
     barrier = pltpu.get_barrier_semaphore()
     for dt, ds in peers:
         pl.semaphore_signal(barrier, inc=1, device_id=peer(dt, ds), device_id_type=MESH)
-    twist_load.start()
-    one_load.start()
-    two_load.start()
-    last_load.start()
-
     def signal_blk(to):
         pl.semaphore_signal(barrier, inc=1, device_id=(turn, to, strip), device_id_type=MESH)
 
@@ -184,44 +189,47 @@
     half = LANES
     outer = length // (2 * half)
     local = ech_raw.shape[2] // 2
-    groups = row_count // 8
-    per_group = 8 // PAIR
-
-    def arrange(group):
+    def stage(group):
+        whole = ech_raw.at[:, pl.ds(0, turns)]
+        pltpu.make_async_copy(whole, whole, load_sem.at[6 + group]).wait()
+
         def fill(to, carry):
             for part in range(2):
                 values = ech_raw[part, to * groups + group].astype(f32)
-                staged[part] = values.reshape(2 * local * 8, half)
+                staged[to, part] = values.reshape(2 * local * 8, half)
+            return carry
+
+        lax.fori_loop(0, turns, fill, 0)
+
+    def pick(step):
+        first = lax.rem(step, per_group) * PAIR
+
+        def fill(to, carry):
             for part in range(2):
-                for row in range(8):
+                for row in range(PAIR):
                     for side in range(2):
-                        value = staged[part, pl.ds(side * 8 + row, local, stride=16), :]
+                        value = staged[to, part, pl.ds(first + side * 8 + row, local, stride=16), :]
                         outbox[
-                            to, group * per_group + row // PAIR, part, row % PAIR, :,
-                            side * half : (side + 1) * half,
+                            to, step, part, row, :, side * half : (side + 1) * half
                         ] = value.astype(bf16)
             return carry
 
         lax.fori_loop(0, turns, fill, 0)
 
-    def send(group):
-        first, end = group * per_group, (group + 1) * per_group
-
-        def start_step(step, carry):
-            for dt, ds in peers:
-                echo_copy(step, dt, ds).start()
-            return carry
-
-        lax.fori_loop(first, end, start_step, 0)
-
-        def keep(step, carry):
-            recv[step, me] = outbox[turn, step]
-            return carry
-
-        lax.fori_loop(first, end, keep, 0)
-
-    echo_load.wait()
-    arrange(0)
+    def send(step):
+        for dt, ds in peers:
+            echo_copy(step, dt, ds).start()
+        recv[step, me] = outbox[turn, step]
+
+    def pick_send(step, carry):
+        pick(step)
+        send(step)
+        return carry
+
+    stage(0)
+    for group in range(1, groups):
+        load_group(group)
+    pick(0)
     pl.semaphore_wait(barrier, len(peers) + jnp.where(blk > 0, 1, 0))
     send(0)
 
@@ -251,9 +259,15 @@
         def _(dz=dz):
             filter_copy(dz).start()
 
+    lax.fori_loop(1, per_group, pick_send, 0)
+    twist_load.start()
+    one_load.start()
+    two_load.start()
+    last_load.start()
+
     for group in range(1, groups):
-        arrange(group)
-        send(group)
+        stage(group)
+        lax.fori_loop(group * per_group, (group + 1) * per_group, pick_send, 0)
     c_ids = lax.broadcasted_iota(jnp.int32, (outer, half), 0)
     lane_ids = lax.broadcasted_iota(jnp.int32, (8, 2 * half), 1)
     k_ids = jnp.where(lane_ids >= half, (lane_ids - half) * (2 * outer) + outer, lane_ids * (2 * outer))
@@ -303,10 +317,8 @@
 
     chunks = outer // CHUNK
 
-    def forward(step, carry):
-        arrived = recv.at[step, pl.ds(0, len(peers))]
-        pltpu.make_async_copy(arrived, arrived, recv_sem.at[step]).wait()
-        rows = [recv[step, :, :, i].reshape(2 * outer, 2 * half) for i in range(PAIR)]
+    def forward_rows(step, picks):
+        rows = [recv[step, :, :, i].reshape(2 * outer, 2 * half) for i in picks]
         rights = []
         for side in range(2):
             lanes = slice(side * half, (side + 1) * half)
@@ -321,59 +333,76 @@
             blocks = []
             for e, value in enumerate((even + odd, even - odd)):
                 tr, ti = twist_ref[2 * e, ids], twist_ref[2 * e + 1, ids]
-                for i in range(PAIR):
-                    lanes = slice(i * half, (i + 1) * half)
+                for k in range(len(picks)):
+                    lanes = slice(k * half, (k + 1) * half)
                     blocks.append(cmul(value[:CHUNK, lanes], value[CHUNK:, lanes], tr, ti))
-            spec[step, chunk] = dot(lefts(blocks), two_ref[0])
+            got = dot(lefts(blocks), two_ref[0])
+            for e in range(2):
+                for k, i in enumerate(picks):
+                    base = (e * len(picks) + k) * CHUNK
+                    spec[step, chunk, e, i] = got[base : base + CHUNK]
+
+    def forward(step, carry):
+        arrived = recv.at[step, pl.ds(0, len(peers))]
+        pltpu.make_async_copy(arrived, arrived, recv_sem.at[step]).wait()
+        forward_rows(step, range(PAIR))
         return carry
 
-    def inverse(step, carry):
-        for chunk in range(chunks):
-            ids = slice(chunk * CHUNK, (chunk + 1) * CHUNK)
+    def inverse_rows(step, picks):
+        count = len(picks)
+        for chunk in range(outer // BACK):
+            ids = slice(chunk * BACK, (chunk + 1) * BACK)
+            first = chunk * BACK % CHUNK
             blocks = []
             for e in range(2):
                 lanes = slice(e * half, (e + 1) * half)
-                for i in range(PAIR):
+                for i in picks:
                     row = step * PAIR + i
                     picked = filt_all[slabs_ref[row], :, e, ids].astype(f32)
                     ur, ui = ramp[row, 0][:1, lanes], ramp[row, 1][:1, lanes]
                     gr, gi = cmul(picked[0], picked[1], ur, ui)
-                    base = (e * PAIR + i) * CHUNK
-                    z = spec[step, chunk, base : base + CHUNK]
+                    z = spec[step, chunk * BACK // CHUNK, e, i, first : first + BACK]
                     blocks.append(cmul(z[:, :half], z[:, half:], gr, gi))
             back = dot(lefts(blocks), two_ref[1])
-            for i in range(PAIR):
+            for k, i in enumerate(picks):
                 row = step * PAIR + i
                 got = []
                 for e in range(2):
-                    base = (e * PAIR + i) * CHUNK
-                    u = back[base : base + CHUNK]
+                    base = (e * count + k) * BACK
+                    u = back[base : base + BACK]
                     got.append(
                         cmul(
                             u[:, :half], u[:, half:],
                             inv_twist[row, 2 * e, ids], inv_twist[row, 2 * e + 1, ids],
                         )
                     )
-                lanes = slice(i * half, (i + 1) * half)
+                lanes = slice(k * half, (k + 1) * half)
                 for part in range(2):
-                    to = slice(part * outer + chunk * CHUNK, part * outer + (chunk + 1) * CHUNK)
+                    to = slice(part * outer + chunk * BACK, part * outer + (chunk + 1) * BACK)
                     for side, value in enumerate((got[0][part] + got[1][part], got[0][part] - got[1][part])):
                         high, low = split(value)
                         middle[side, 0, to, lanes] = high
                         middle[side, 1, to, lanes] = low
-        return lax.fori_loop(step, step + 1, inverse_two, carry)
-
-    def inverse_two(step, carry):
+
+    def image_rows(step, picks):
         rows = outer // strips
+        width = len(picks) * half
         for side in range(2):
-            high, low = middle[side, 0], middle[side, 1]
+            high, low = middle[side, 0, :, :width], middle[side, 1, :, :width]
             res = dot(last_ref[side], jnp.concatenate([high, high, low], 0))
-            for i in range(PAIR):
+            for k, i in enumerate(picks):
                 place = lax.rem(step, 8 // PAIR) * PAIR + i + 8 * side
                 for part in range(2):
                     out_ref[part, step // (8 // PAIR), pl.ds(place, rows, stride=16), :] = res[
-                        part * rows : (part + 1) * rows, i * half : (i + 1) * half
+                        part * rows : (part + 1) * rows, k * half : (k + 1) * half
                     ]
+
+    def inverse(step, carry):
+        inverse_rows(step, range(PAIR))
+        return lax.fori_loop(step, step + 1, image, carry)
+
+    def image(step, carry):
+        image_rows(step, range(PAIR))
         return carry
 
     def both(step, carry):
@@ -430,7 +459,7 @@
             pltpu.VMEM((slab_local * blks, 2, 2, outer, half), bf16),
             pltpu.VMEM((row_count, 4, outer, half), f32),
             pltpu.VMEM((row_count, 2, 8, 2 * half), f32),
-            pltpu.VMEM((pairs, outer // CHUNK, 2 * PAIR * CHUNK, 2 * half), f32),
+            pltpu.VMEM((pairs, outer // CHUNK, 2, PAIR, CHUNK, 2 * half), f32),
             pltpu.VMEM((2, 2, 2 * outer, 2 * half), bf16),
             pltpu.VMEM(tables[0].shape, bf16),
             pltpu.VMEM(tables[1].shape, bf16),
@@ -438,7 +467,7 @@
             pltpu.VMEM(tables[3].shape[1:], bf16),
             pltpu.VMEM(shaped.shape, bf16),
             pltpu.VMEM(response.shape, bf16),
-            pltpu.VMEM((2, 16 * local, half), f32),
+            pltpu.VMEM((turns, 2, 16 * local, half), f32),
             pltpu.VMEM((turns, pairs, 2, PAIR, local, 2 * half), bf16),
             pltpu.SemaphoreType.DMA((1,)),
             pltpu.SemaphoreType.DMA((pairs,)),
@@ -446,7 +475,7 @@
             pltpu.SemaphoreType.DMA((blks,)),
             pltpu.SemaphoreType.DMA((1,)),
             pltpu.SemaphoreType.DMA((1,)),
-            pltpu.SemaphoreType.DMA((6,)),
+            pltpu.SemaphoreType.DMA((6 + row_count // 8,)),
         ],
         compiler_params=pltpu.CompilerParams(
             collective_id=0, has_side_effects=True, vmem_limit_bytes=56 * 1024 * 1024

time: 31.6 us -> 31.5 us (level)
  no operation moved by 1% of the time
where the time goes in v5:
time: 31.5 us; the launch traced here: 31.2 us
  Pallas kernels  29.9 us (95%)
  local copies, waits for them, and re-layouts  1.32 us (4%)
    pallas_call x1, Pallas kernels, per_device(): pl.pallas_call(functools.partial(body, turns, blks, strips, length), out_...  29.9 us
    unnamed x1, local copies, waits for them, and re-layouts  1.32 us

profile of v5, /device:TPU:0, one launch (start us, length us, event | category | flops | bytes accessed | tf_op | source)
XLA Modules:
  0.0 31.2 jit_solution(13866296123714803991)
XLA Ops:
  0.0 29.9 %shard_map.82 = f32[2,2,1024,128]{3,2,1,0:T(8,128)S(1)} custom-call(s32[16]{0:T(128)} %shifts_ref.1, s32[16]{0:T(128)} %slabs_ref.1, bf16[2,8,32,8,128]{4,3,2,1,0:T(8,128)(2,1)} %bitcast.14, bf16[2,512,128]{2,1,0:T(8,128)(2,1)} %bitcast.15, bf16[2,256,512]{2,1,0:T(8,128)(2,1)} %constant.8.clone.one_hbm, bf16[2,768,256]{2,1,0:T(8,128)(2,1)} %constant.9.clone.two_hbm, ...), custom_call_target="tpu_custom_call" | custom-call | tf_op jit(solution)/shard_map/pallas_call | solution.py:452
  29.9 1.3 %copy.11 = f32[2,16,16384]{2,1,0:T(8,128)} copy(f32[2,16,16384]{2,1,0:T(8,128)S(1)} %bitcast.13) | data formatting | bytes 4194304

commit v6 on v5

--- a/solution.py
+++ b/solution.py
@@ -122,7 +122,7 @@
     peers = [
         (dt, ds) for dt in range(turns) for ds in range(strips) if (dt, ds) != (0, 0)
     ]
-    peers.sort(key=lambda p: (p[1] == 0, p[0] < 2, p))
+    peers.sort(key=lambda p: (p[1] == 0, p[0] % 2, p[0] < 2, p))
 
     def peer(dt, ds):
         to = lax.rem(turn - core + (dt // 2) * 2, turns) + lax.rem(core + dt, 2)
@@ -265,6 +265,20 @@
     two_load.start()
     last_load.start()
 
+    @pl.when(blk < blks - 1)
+    def _():
+        pl.semaphore_wait(barrier, 1)
+
+        @pl.when(blk > 0)
+        def _():
+            signal_blk(blk - 1)
+
+        for dz in range(1, blks):
+
+            @pl.when(blk + dz < blks)
+            def _(dz=dz):
+                filter_copy(dz).start()
+
     for group in range(1, groups):
         stage(group)
         lax.fori_loop(group * per_group, (group + 1) * per_group, pick_send, 0)
@@ -285,20 +299,6 @@
         ramp[row, 0] = ur
         ramp[row, 1] = -ui
         return carry
-
-    @pl.when(blk < blks - 1)
-    def _():
-        pl.semaphore_wait(barrier, 1)
-
-        @pl.when(blk > 0)
-        def _():
-            signal_blk(blk - 1)
-
-        for dz in range(1, blks):
-
-            @pl.when(blk + dz < blks)
-            def _(dz=dz):
-                filter_copy(dz).start()
 
     twist_load.wait()
     lax.fori_loop(0, row_count, prepare, 0)

time: 31.5 us -> 31.2 us (level)
  no operation moved by 1% of the time
where the time goes in v6:
time: 31.2 us; the launch traced here: 31 us
  Pallas kernels  29.7 us (95%)
  local copies, waits for them, and re-layouts  1.32 us (4%)
    pallas_call x1, Pallas kernels, per_device(): pl.pallas_call(functools.partial(body, turns, blks, strips, length), out_...  29.7 us
    unnamed x1, local copies, waits for them, and re-layouts  1.32 us

profile of v6, /device:TPU:0, one launch (start us, length us, event | category | flops | bytes accessed | tf_op | source)
XLA Modules:
  0.0 31.0 jit_solution(12576467877293796976)
XLA Ops:
  0.0 29.7 %shard_map.82 = f32[2,2,1024,128]{3,2,1,0:T(8,128)S(1)} custom-call(s32[16]{0:T(128)} %shifts_ref.1, s32[16]{0:T(128)} %slabs_ref.1, bf16[2,8,32,8,128]{4,3,2,1,0:T(8,128)(2,1)} %bitcast.14, bf16[2,512,128]{2,1,0:T(8,128)(2,1)} %bitcast.15, bf16[2,256,512]{2,1,0:T(8,128)(2,1)} %constant.8.clone.one_hbm, bf16[2,768,256]{2,1,0:T(8,128)(2,1)} %constant.9.clone.two_hbm, ...), custom_call_target="tpu_custom_call" | custom-call | tf_op jit(solution)/shard_map/pallas_call | solution.py:452
  29.7 1.3 %copy.11 = f32[2,16,16384]{2,1,0:T(8,128)} copy(f32[2,16,16384]{2,1,0:T(8,128)S(1)} %bitcast.13) | data formatting | bytes 4194304

commit v7 on v6

--- a/solution.py
+++ b/solution.py
@@ -399,9 +399,6 @@
 
     def inverse(step, carry):
         inverse_rows(step, range(PAIR))
-        return lax.fori_loop(step, step + 1, image, carry)
-
-    def image(step, carry):
         image_rows(step, range(PAIR))
         return carry
 

time: 31.2 us -> 31.2 us (level)
  no operation moved by 1% of the time
where the time goes in v7:
time: 31.2 us; the launch traced here: 31 us
  Pallas kernels  29.7 us (95%)
  local copies, waits for them, and re-layouts  1.32 us (4%)
    pallas_call x1, Pallas kernels, per_device(): pl.pallas_call(functools.partial(body, turns, blks, strips, length), out_...  29.7 us
    unnamed x1, local copies, waits for them, and re-layouts  1.32 us

profile of v7, /device:TPU:0, one launch (start us, length us, event | category | flops | bytes accessed | tf_op | source)
XLA Modules:
  0.0 31.0 jit_solution(17847734251448072876)
XLA Ops:
  0.0 29.7 %shard_map.82 = f32[2,2,1024,128]{3,2,1,0:T(8,128)S(1)} custom-call(s32[16]{0:T(128)} %shifts_ref.1, s32[16]{0:T(128)} %slabs_ref.1, bf16[2,8,32,8,128]{4,3,2,1,0:T(8,128)(2,1)} %bitcast.14, bf16[2,512,128]{2,1,0:T(8,128)(2,1)} %bitcast.15, bf16[2,256,512]{2,1,0:T(8,128)(2,1)} %constant.8.clone.one_hbm, bf16[2,768,256]{2,1,0:T(8,128)(2,1)} %constant.9.clone.two_hbm, ...), custom_call_target="tpu_custom_call" | custom-call | tf_op jit(solution)/shard_map/pallas_call | solution.py:449
  29.7 1.3 %copy.11 = f32[2,16,16384]{2,1,0:T(8,128)} copy(f32[2,16,16384]{2,1,0:T(8,128)S(1)} %bitcast.13) | data formatting | bytes 4194304
